TPU v7x, 128 devices: a whole 4x4x4 slice. The times are simulated.
128 devices in a mesh: cuts: 8 (over z, x_lo), row: 16 (over x_hi, y, core).
Axes of the slice: x: 4 (x_hi: 2, x_lo: 2; x = x_hi * 2 + x_lo), y: 4, z: 4, core: 2. Of those that a mesh axis runs over, the one named last changes fastest.
Arguments:
- eigvecs: float32 [16384, 4096], P('row', 'cuts'), may hold values from -1.2 to 1.2
- slice_counts: int32 [8], P('cuts'), may hold values from 256 to 512, as said below
- occ_index: int32 [4096], P('cuts'), may hold values from 0 to 63
- occ_levels: float32 [64], replicated, may hold values from 0 to 1
Outputs:
- slab: float32 [4096, 16384], P('cuts', 'row')
Inputs may be any that keep to these rules, and one draw needn't show every extreme that they name: `slice_counts`: some slice holds exactly 512 eigenvalues in every draw; the others at least half of that.
All inputs are finite; a program needn't handle non-finite values.
Results may differ from a plain program's by a relative error of at most 0.000062.
Values sent between devices are 32-bit elements; how exact they have to be, the bound alone decides.
A program may use at most 128 MiB of HBM per device.

v0:
```python
import jax
import jax.numpy as jnp
from jax import lax
from jax.sharding import Mesh
from jax.sharding import PartitionSpec as P

BLOCK = 1024
SLAB_SUB = 256
CUTS = ("cuts_0", "cuts_1")


def sum_by_axis(total, axes):
    for axis in axes:
        total = lax.psum_scatter(total, axis, scatter_dimension=0, tiled=True)
    return total


def shards(eigvecs, slice_counts, occ_index, occ_levels):
    row_count = eigvecs.shape[0]
    slot_count = eigvecs.shape[1]
    level_ids = jnp.arange(occ_levels.shape[0], dtype=jnp.int32)
    one_hot = (occ_index[:, None] == level_ids[None, :]).astype(jnp.float32)
    values = jnp.dot(one_hot, occ_levels, precision=lax.Precision.HIGHEST)
    live = jnp.arange(slot_count, dtype=jnp.int32) < slice_counts[0]
    weights = jnp.where(live, values, jnp.float32(0.0))
    local_blocks = eigvecs.reshape(row_count // BLOCK, BLOCK, slot_count)[:, :SLAB_SUB, :]
    local_rows = local_blocks.reshape(-1, slot_count) * weights[None, :]
    gathered = lax.all_gather(local_rows, "row", axis=0, tiled=True)
    return sum_by_axis(
        lax.dot_general(
            gathered,
            eigvecs,
            (((1,), (1,)), ((), ())),
            precision=lax.Precision.HIGHEST,
            preferred_element_type=jnp.float32,
        ),
        CUTS,
    )


def solution(mesh):
    finer = Mesh(mesh.devices.reshape(4, 2, mesh.shape["row"]), ("cuts_0", "cuts_1", "row"))
    in_specs = (P("row", CUTS), P(CUTS), P(CUTS), P())
    out_specs = P(CUTS, "row")
    return jax.shard_map(
        shards, mesh=finer, in_specs=in_specs, out_specs=out_specs, check_vma=False
    )
```

profile of v0, /device:TPU:1, one launch (start us, length us, event | category | flops | bytes accessed | tf_op | source)
XLA Modules:
  0.0 329.1 jit_solution(11867658746482311696)
XLA Ops:
  6.5 0.0 copy-start
  6.5 0.0 all-gather.2.cloned.1.call-start
  7.2 0.0 copy-done
  7.2 1.0 fusion.1
  8.2 1.9 fusion
  10.1 0.0 all-gather.2.cloned.1.call-update
  10.1 0.0 reduce-scatter.3.cloned.1.call-start
  10.2 76.3 %all-gather.2.cloned.1.call-done = f32[4096,512]{1,0:T(8,128)} async-done(((f32[256,512]{1,0:T(8,128)}), f32[4096,512]{1,0:T(8,128)}) %all-gather.2.cloned.1.call-update) | async-done | bytes 8388624 | tf_op jit(solution)/shard_map/all_gather | solution.py:28
  86.4 31.7 %fusion.5 = f32[4096,1024]{1,0:T(8,128)} fusion(f32[4096,512]{1,0:T(8,128)} %all-gather.2.cloned.1.call-done, f32[1024,512]{1,0:T(8,128)} %param.4), kind=kOutput, calls=%fused_computation.8 | convolution fusion | flops 25769803776 | bytes 27262976 | tf_op jit(solution)/shard_map/dot_general | solution.py:30
  118.1 0.0 reduce-scatter.3.cloned.1.call-update
  118.1 0.0 reduce-scatter.5.cloned.1.call-start
  118.2 145.6 %reduce-scatter.3.cloned.1.call-done = f32[1024,1024]{1,0:T(8,128)} async-done(((f32[4096,1024]{1,0:T(8,128)}), f32[1024,1024]{1,0:T(8,128)}) %reduce-scatter.3.cloned.1.call-update) | async-done | bytes 4194320 | tf_op jit(solution)/shard_map/reduce_scatter | solution.py:14
  263.8 0.0 reduce-scatter.5.cloned.1.call-update
  263.8 58.8 %reduce-scatter.5.cloned.1.call-done = f32[512,1024]{1,0:T(8,128)} async-done(((f32[1024,1024]{1,0:T(8,128)}), f32[512,1024]{1,0:T(8,128)}) %reduce-scatter.5.cloned.1.call-update) | async-done | bytes 2097168 | tf_op jit(solution)/shard_map/reduce_scatter | solution.py:14
  (1 shorter events, 0.0 us)
Async XLA Ops:
  6.5 0.7 copy-start
  6.5 79.9 %all-gather.2.cloned.1.call-start = ((), (), s32[]{:S(2)}) async-start(), calls=%async_computation.2 | async-start | bytes 8912896 | tf_op jit(solution)/shard_map/all_gather | solution.py:28
  10.1 253.7 %reduce-scatter.3.cloned.1.call-start = ((), (), s32[]{:S(2)}) async-start(), calls=%async_computation.3 | async-start | bytes 20971520 | tf_op jit(solution)/shard_map/reduce_scatter | solution.py:14
  118.1 204.5 %reduce-scatter.5.cloned.1.call-start = ((), (), s32[]{:S(2)}) async-start(), calls=%async_computation.4 | async-start | bytes 6291456 | tf_op jit(solution)/shard_map/reduce_scatter | solution.py:14
Sparse Core Ops, SparseCore 0:
  10.2 76.1 all-gather.1
  118.3 145.5 reduce-scatter.2
  266.2 56.3 reduce-scatter.4
where the time goes:
time: 329 us
  waiting for transfers between devices  281 us (85%)
  matrix products  32.7 us (10%)
  between operations  13.8 us (4%)
    reduce_scatter x2, waiting for transfers between devices, sum_by_axis(): total = lax.psum_scatter(total, axis, scatter_dimension=0, tiled=True)  204 us
    all_gather x1, waiting for transfers between devices, shards(): gathered = lax.all_gather(local_rows, 'row', axis=0, tiled=True)  76.3 us
    dot_general x1, matrix products, shards(): lax.dot_general(gathered, eigvecs, (((1,), (1,)), ((), ())), precision=la...  31.7 us
  transfers between devices with their start and end apart: 3, of which 3 were waited for; matrix products, arithmetic and copies ran while one was open for 0% of the time, Pallas kernels for 0%

commit v1 on v0

--- a/solution.py
+++ b/solution.py
@@ -25,7 +25,9 @@
     weights = jnp.where(live, values, jnp.float32(0.0))
     local_blocks = eigvecs.reshape(row_count // BLOCK, BLOCK, slot_count)[:, :SLAB_SUB, :]
     local_rows = local_blocks.reshape(-1, slot_count) * weights[None, :]
-    gathered = lax.all_gather(local_rows, "row", axis=0, tiled=True)
+    gathered = jnp.concatenate(
+        lax.all_to_all(jnp.stack([local_rows] * lax.axis_size("row")), "row", 0, 0), axis=0
+    )
     return sum_by_axis(
         lax.dot_general(
             gathered,

time: 329 us -> 357 us (1.085)
  blocking collectives: 0 us -> 104 us
  waiting for transfers between devices: 281 us -> 206 us
    all_to_all x0 -> x1, blocking collectives: none -> 104 us  [shards(): lax.all_to_all(jnp.stack([local_rows] * lax.axis_size('row')), 'row', 0, 0)]
    all_gather x1 -> x0, waiting for transfers between devices: 76.3 us -> none  [shards(): gathered = lax.all_gather(local_rows, 'row', axis=0, tiled=True)]
  transfers between devices with their start and end apart: 3 -> 2, of which waited for: 3 -> 2; matrix products, arithmetic and copies ran while one was open for 0% -> 0% of each run, Pallas kernels for 0% -> 0%
where the time goes in v1:
time: 357 us
  waiting for transfers between devices  206 us (58%)
  blocking collectives  104 us (29%)
  matrix products  30.9 us (9%)
  between operations  14.1 us (4%)
    reduce_scatter x2, waiting for transfers between devices, sum_by_axis(): total = lax.psum_scatter(total, axis, scatter_dimension=0, tiled=True)  206 us
    all_to_all x1, blocking collectives, shards(): lax.all_to_all(jnp.stack([local_rows] * lax.axis_size('row')), 'row', 0, 0)  104 us
    dot_general x1, matrix products, shards(): lax.dot_general(gathered, eigvecs, (((1,), (1,)), ((), ())), precision=la...  29.9 us
  transfers between devices with their start and end apart: 2, of which 2 were waited for; matrix products, arithmetic and copies ran while one was open for 0% of the time, Pallas kernels for 0%

profile of v1, /device:TPU:1, one launch (start us, length us, event | category | flops | bytes accessed | tf_op | source)
XLA Modules:
  0.0 357.2 jit_solution(1778164764065327968)
XLA Ops:
  6.5 0.0 copy-start
  6.5 0.0 reduce-scatter.3.cloned.1.call-start
  7.2 0.0 copy-done
  7.2 1.0 fusion.1
  8.2 1.1 fusion
  9.3 1.1 stack.5
  10.4 0.0 copy-start.1
  10.4 103.8 %all_to_all.5 = f32[16,256,512]{2,1,0:T(8,128)S(1)} all-to-all(f32[16,256,512]{2,1,0:T(8,128)S(1)} %stack.5), channel_id=1, replica_groups=mesh['cuts_0'=4,'cuts_1'=2,'row'=16] {'row'}, dimensions={0} | all-to-all | bytes 16777216 | tf_op jit(solution)/shard_map/all_to_all | solution.py:29
  114.2 0.0 copy-done.1
  114.2 29.9 %fusion.5 = f32[4096,1024]{1,0:T(8,128)} fusion(f32[4096,512]{1,0:T(8,128)S(1)} %bitcast.12, f32[1024,512]{1,0:T(8,128)S(1)} %copy-done.1), kind=kOutput, calls=%fused_computation.8 | convolution fusion | flops 25769803776 | bytes 27262976 | tf_op jit(solution)/shard_map/dot_general | solution.py:32
  144.1 0.0 reduce-scatter.3.cloned.1.call-update
  144.1 0.0 reduce-scatter.5.cloned.1.call-start
  144.2 147.4 %reduce-scatter.3.cloned.1.call-done = f32[1024,1024]{1,0:T(8,128)} async-done(((f32[4096,1024]{1,0:T(8,128)}), f32[1024,1024]{1,0:T(8,128)}) %reduce-scatter.3.cloned.1.call-update) | async-done | bytes 4194320 | tf_op jit(solution)/shard_map/reduce_scatter | solution.py:14
  291.5 0.0 reduce-scatter.5.cloned.1.call-update
  291.6 58.8 %reduce-scatter.5.cloned.1.call-done = f32[512,1024]{1,0:T(8,128)} async-done(((f32[1024,1024]{1,0:T(8,128)}), f32[512,1024]{1,0:T(8,128)}) %reduce-scatter.5.cloned.1.call-update) | async-done | bytes 2097168 | tf_op jit(solution)/shard_map/reduce_scatter | solution.py:14
  (1 shorter events, 0.0 us)
Async XLA Ops:
  6.5 0.7 copy-start
  6.5 285.0 %reduce-scatter.3.cloned.1.call-start = ((), (), s32[]{:S(2)}) async-start(), calls=%async_computation.3 | async-start | bytes 20971520 | tf_op jit(solution)/shard_map/reduce_scatter | solution.py:14
  10.4 103.8 %copy-start.1 = (f32[1024,512]{1,0:T(8,128)S(1)}, f32[1024,512]{1,0:T(8,128)}, u32[]{:S(2)}) copy-start(f32[1024,512]{1,0:T(8,128)} %param.4) | copy-start | bytes 6291460
  144.1 206.2 %reduce-scatter.5.cloned.1.call-start = ((), (), s32[]{:S(2)}) async-start(), calls=%async_computation.4 | async-start | bytes 6291456 | tf_op jit(solution)/shard_map/reduce_scatter | solution.py:14
Sparse Core Ops, SparseCore 0:
  144.2 147.2 reduce-scatter.2
  293.9 56.3 reduce-scatter.4
